TPU v7x, 32 devices: a whole 2x2x4 slice. The times are simulated.
32 devices in a mesh: tp: 4 (over z), cp: 2 (over x), dp: 4 (over y, core).
Axes of the slice: x: 2, y: 2, z: 4, core: 2. Of those that a mesh axis runs over, the one named last changes fastest.
Arguments:
- tokens: bfloat16 [2048, 7168], P(('dp', 'tp', 'cp')), parts along dimension 0, may hold values from -6 to 6
- router: bfloat16 [7168, 4], replicated, may hold values from -0.0625 to 0.0625
- gate_weight: bfloat16 [4, 7168, 1024], P('cp', None, 'tp'), may hold values from -0.0625 to 0.0625
- up_weight: bfloat16 [4, 7168, 1024], P('cp', None, 'tp'), may hold values from -0.0625 to 0.0625
- down_weight: bfloat16 [4, 1024, 7168], P('cp', 'tp'), may hold values from -0.1875 to 0.1875
- expert_ids: int32 [2048, 2], P(('dp', 'tp', 'cp')), parts along dimension 0, may hold values from 0 to 3, as said below
- slot_index: int32 [2048, 2], P(('dp', 'tp', 'cp')), parts along dimension 0, may hold values from -1 to 1, as said below
Outputs:
- moe_out: bfloat16 [2048, 7168], P(('dp', 'tp', 'cp')), parts along dimension 0
There are 4 independent parts, one for each index of `dp`. A program takes and returns all parts, laid end to end along the dimension named above; an argument that names none is the same for every part. Nothing has to cross between parts.
Inputs may be any that keep to these rules, and one draw needn't show every extreme that they name: `expert_ids`: each row names 2 different experts in rising order; in every part one expert is named by 32 or more rows of every block. slot_index[t, k] is the number of earlier copies to expert expert_ids[t, k] within token t's block (rows in order, then k in order) when that is below 2, else -1.
All inputs are finite; a program needn't handle non-finite values.
Results may differ from a plain program's by a relative error of at most 0.012.
Values may be sent and summed in bfloat16 or wider, within the bound.
A program may use at most 64 MiB of HBM per device.

v0:
```python
import jax
import jax.numpy as jnp
from jax import lax
from jax.sharding import PartitionSpec as P

CAP_DEV = 2


route_scale = 2.5


def body(tokens, router, gate_weight, up_weight, down_weight, expert_ids, slot_index):
    experts = router.shape[1]
    local_experts = gate_weight.shape[0]
    model_width = tokens.shape[1]
    tensor_size = lax.axis_size("tp")
    context_size = lax.axis_size("cp")
    logits = jnp.dot(tokens, router, preferred_element_type=jnp.float32)
    affinity = jax.nn.sigmoid(logits)
    chosen = jnp.take_along_axis(affinity, expert_ids, axis=1)
    gate_share = route_scale * chosen / jnp.sum(chosen, axis=1, keepdims=True)
    target = jnp.where(slot_index >= 0, expert_ids * CAP_DEV + slot_index, -1)
    columns = jnp.arange(experts * CAP_DEV, dtype=jnp.int32)
    matches = (target[:, :, None] == columns[None, None, :]).astype(jnp.float32)
    placing = jnp.sum(matches, axis=1)
    mixing = jnp.sum(matches * gate_share[:, :, None], axis=1)
    outgoing = jnp.dot(placing.T.astype(jnp.bfloat16), tokens, preferred_element_type=jnp.float32)
    outgoing = outgoing.astype(jnp.bfloat16).reshape(experts, CAP_DEV, model_width)
    copies = jnp.broadcast_to(outgoing[None], (tensor_size,) + outgoing.shape)
    copies = copies.reshape(tensor_size * experts, CAP_DEV, model_width)
    received = lax.all_to_all(copies, ("tp", "cp"), split_axis=0, concat_axis=0, tiled=True)
    slot_count = received.shape[1]
    sources = received.shape[0] // local_experts
    arranged = received.reshape(sources, local_experts, slot_count, model_width)
    arranged = jnp.transpose(arranged, (1, 0, 2, 3)).reshape(
        local_experts, sources * slot_count, model_width
    )
    gate_part = jnp.einsum(
        "esd,edf->esf", arranged, gate_weight, preferred_element_type=jnp.float32
    )
    up_part = jnp.einsum("esd,edf->esf", arranged, up_weight, preferred_element_type=jnp.float32)
    hidden = (jax.nn.silu(gate_part) * up_part).astype(jnp.bfloat16)
    partial_value = (
        jnp.einsum("esf,efd->esd", hidden, down_weight, preferred_element_type=jnp.float32)
        .astype(jnp.bfloat16)
        .reshape(local_experts, sources, slot_count, model_width)
    )
    partial_value = jnp.transpose(partial_value, (1, 0, 2, 3)).reshape(
        sources * local_experts, slot_count, model_width
    )
    slot_count = partial_value.shape[1]
    returned = lax.all_to_all(partial_value, ("tp", "cp"), split_axis=0, concat_axis=0, tiled=True)
    grouped = returned.reshape(tensor_size, context_size * local_experts, slot_count, model_width)
    expert_out = jnp.sum(grouped.astype(jnp.float32), axis=0)
    combined = jnp.dot(
        mixing, expert_out.reshape(experts * CAP_DEV, model_width), precision=lax.Precision.HIGHEST
    )
    return combined.astype(jnp.bfloat16)


def solution(mesh):
    in_specs = (
        P(("dp", "tp", "cp"), None),
        P(),
        P("cp", None, "tp"),
        P("cp", None, "tp"),
        P("cp", "tp", None),
        P(("dp", "tp", "cp"), None),
        P(("dp", "tp", "cp"), None),
    )
    out_specs = P(("dp", "tp", "cp"), None)
    return jax.shard_map(body, mesh=mesh, in_specs=in_specs, out_specs=out_specs, check_vma=False)
```

profile of v0, /device:TPU:0, one launch (start us, length us, event | category | flops | bytes accessed | tf_op | source)
XLA Modules:
  0.0 57.4 jit_solution(2514599024744497666)
XLA Ops:
  0.0 0.0 copy-start
  0.0 0.8 %bitcast_or_fusion = s32[64,2,1]{0,1,2:T(2,128)S(1)} fusion(s32[64,2]{0,1:T(2,128)} %param.12), kind=kLoop, calls=%fused_computation.24 | loop fusion | flops 1024 | bytes 1024 | tf_op jit(solution)/shard_map/jit(take_along_axis)/gather | solution.py:20
  0.8 0.7 %compare_select_fusion.1 = s32[64,2]{0,1:T(2,128)S(1)} fusion(s32[64,2]{0,1:T(2,128)} %param.13, s32[64,2]{0,1:T(2,128)} %param.12), kind=kLoop, calls=%fused_computation.23 | loop fusion | flops 512 | bytes 1536 | tf_op jit(solution)/shard_map/jit(_where)/select_n | solution.py:22
  1.5 0.1 copy.50
  1.6 0.1 reshape.52
  1.7 0.0 copy-done
  1.7 1.2 %fusion.3 = f32[64,4]{0,1:T(4,128)S(1)} fusion(bf16[64,7168]{1,0:T(8,128)(2,1)S(1)} %copy-done, bf16[7168,4]{0,1:T(4,128)(2,1)} %param.8), kind=kOutput, calls=%fused_computation.9 | convolution fusion | flops 3670784 | bytes 975872 | tf_op jit(solution)/shard_map/dot_general | solution.py:18
  2.9 1.5 %gather_fusion = f32[128]{0:T(128)S(1)} fusion(f32[64,4]{0,1:T(4,128)S(1)} %fusion.3, s32[128]{0:T(128)S(1)} %reshape.52), kind=kCustom, calls=%fused_computation | custom fusion | bytes 2048 | tf_op jit(solution)/shard_map/jit(take_along_axis)/gather | solution.py:20
  4.4 0.1 reshape.55
  4.6 0.1 copy.51
  4.7 0.2 convolution_convert_fusion.2
  4.9 0.1 broadcast_in_dim.21
  5.0 0.2 broadcast_in_dim.22
  5.2 20.3 %all_to_all.10 = bf16[16,2,7168]{2,1,0:T(2,128)(2,1)S(1)} all-to-all(bf16[16,2,7168]{2,1,0:T(2,128)(2,1)S(1)} %bitcast.26), channel_id=1, replica_groups=mesh['tp'=4,'cp'=2,'dp'=4] {'tp','cp'}, dimensions={0} | all-to-all | bytes 917504 | tf_op jit(solution)/shard_map/all_to_all | solution.py:31
  25.5 0.3 copy.52
  25.8 0.2 reshape.47
  26.0 4.2 %fusion.13 = f32[2,16,256]{2,1,0:T(8,128)S(1)} fusion(bf16[2,16,7168]{2,1,0:T(8,128)(2,1)S(1)} %reshape.47, bf16[2,7168,256]{2,1,0:T(8,128)(2,1)} %param.9), kind=kOutput, calls=%fused_computation.28 | convolution fusion | flops 117440512 | bytes 7831552 | tf_op jit(solution)/shard_map/esd,edf->esf/dot_general | solution.py:38
  30.2 7.3 %convolution_convert_fusion.1 = bf16[2,16,7168]{2,1,0:T(8,128)(2,1)S(1)} fusion(bf16[2,256,7168]{2,1,0:T(8,128)(2,1)} %param.11, bf16[2,16,7168]{2,1,0:T(8,128)(2,1)S(1)} %reshape.47, bf16[2,7168,256]{2,1,0:T(8,128)(2,1)} %param.10, f32[2,16,256]{2,1,0:T(8,128)S(1)} %fusion.13), kind=kOutput, calls=%fused_computation.2 | convolution fusion | flops 235159552 | bytes 15630336 | tf_op jit(solution)/shard_map/esf,efd->esd/dot_general | solution.py:44
  37.4 0.2 reshape.48
  37.6 0.3 copy.53
  37.9 16.3 %all_to_all.11 = bf16[16,2,7168]{2,1,0:T(2,128)(2,1)S(1)} all-to-all(bf16[16,2,7168]{2,1,0:T(2,128)(2,1)S(1)} %bitcast.25), channel_id=1, replica_groups=mesh['tp'=4,'cp'=2,'dp'=4] {'tp','cp'}, dimensions={0} | all-to-all | bytes 917504 | tf_op jit(solution)/shard_map/all_to_all | solution.py:52
  54.2 0.5 convert_reduce_fusion
  54.7 0.2 reshape.50
  54.9 2.6 %convolution_convert_fusion = bf16[64,7168]{1,0:T(8,128)(2,1)} fusion(f32[64,8]{0,1:T(8,128)S(1)} %get-tuple-element.6, f32[8,7168]{1,0:T(8,128)S(1)} %reshape.50), kind=kOutput, calls=%fused_computation.1 | convolution fusion | flops 44498944 | bytes 1148928 | tf_op jit(solution)/shard_map/dot_general | solution.py:55
  (5 shorter events, 0.1 us)
Async XLA Ops:
  0.0 1.7 %copy-start = (bf16[64,7168]{1,0:T(8,128)(2,1)S(1)}, bf16[64,7168]{1,0:T(8,128)(2,1)}, u32[]{:S(2)}) copy-start(bf16[64,7168]{1,0:T(8,128)(2,1)} %param.7) | copy-start | bytes 2752516
  2.9 1.8 %copy-start.1 = (s32[64,2]{0,1:T(2,128)S(1)}, s32[64,2]{0,1:T(2,128)}, u32[]{:S(2)}) copy-start(s32[64,2]{0,1:T(2,128)} %param.12) | copy-start | bytes 1540
where the time goes:
time: 57.7 us; the launch traced here: 57.4 us
  blocking collectives  36.6 us (63%)
  matrix products  15.4 us (27%)
  local copies, waits for them, and re-layouts  3.42 us (6%)
  other arithmetic  1.96 us (3%)
    all_to_all x1, blocking collectives, body(): lax.all_to_all(copies, ('tp', 'cp'), split_axis=0, concat_axis=0, tiled=T...  20.3 us
    all_to_all x1, blocking collectives, body(): lax.all_to_all(partial_value, ('tp', 'cp'), split_axis=0, concat_axis=0,...  16.3 us
    dot_general x1, matrix products, body(): jnp.einsum('esf,efd->esd', hidden, down_weight, preferred_element_type=jn...  7.26 us
    dot_general x1, matrix products, body(): jnp.einsum('esd,edf->esf', arranged, gate_weight, preferred_element_type=...  4.16 us
    dot_general x1, matrix products, body(): jnp.dot(mixing, expert_out.reshape(experts * CAP_DEV, model_width), preci...  2.56 us
    gather x5, local copies, waits for them, and re-layouts, body(): chosen = jnp.take_along_axis(affinity, expert_ids, axis=1)  1.97 us
    dot_general x1, matrix products, body(): logits = jnp.dot(tokens, router, preferred_element_type=jnp.float32)  1.16 us

commit v1 on v0

v1 whole, which is shorter than its diff:
```python
import functools

import jax
import jax.numpy as jnp
from jax import lax
from jax.experimental import pallas as pl
from jax.experimental.pallas import tpu as pltpu
from jax.sharding import PartitionSpec as P

CAP_DEV = 2
ROUTE_SCALE = 2.5
MESH = pl.DeviceIdType.MESH
NT = (((1,), (1,)), ((), ()))
TN = (((0,), (0,)), ((), ()))


def rows_of(ref, c):
    pieces = [ref[c, i].astype(jnp.float32) for i in range(ref.shape[1])]
    return jnp.concatenate(pieces, axis=0).astype(jnp.bfloat16)


def kernel(
    n_tp, n_cp, nc,
    tok_hbm, rt_hbm, ids_ref, slot_ref, wg_hbm, wu_hbm, wd_hbm,
    out_hbm,
    tok, rt, wg, wu, wd, xs, xr, ps, pr, ob,
    in_sem, wsem, osem, s1, r1, s2, r2,
):
    n = n_tp * n_cp
    my_z, my_x = lax.axis_index("tp"), lax.axis_index("cp")
    me = my_z * n_cp + my_x
    local, width, ff = wg.shape
    rpp = xr.shape[2]
    dc = width // nc
    slots = n_cp * rpp

    tok_copy = pltpu.make_async_copy(tok_hbm, tok, in_sem.at[0])
    tok_copy.start()
    rt_copy = pltpu.make_async_copy(rt_hbm, rt, in_sem.at[1])
    rt_copy.start()

    def peer(j):
        other = lax.rem(me + j, n)
        return other, {"tp": other // n_cp, "cp": lax.rem(other, n_cp)}

    barrier = pltpu.get_barrier_semaphore()
    for j in range(1, n):
        pl.semaphore_signal(barrier, inc=1, device_id=peer(j)[1], device_id_type=MESH)

    up_copies, down_copies = [], []
    for c in range(nc):
        cols = pl.ds(c * dc, dc)
        pair = [
            pltpu.make_async_copy(wg_hbm.at[:, cols, :], wg.at[:, cols, :], wsem.at[0, c]),
            pltpu.make_async_copy(wu_hbm.at[:, cols, :], wu.at[:, cols, :], wsem.at[1, c]),
        ]
        for copy in pair:
            copy.start()
        up_copies.append(pair)
    for c in range(nc):
        cols = pl.ds(c * dc, dc)
        copy = pltpu.make_async_copy(wd_hbm.at[:, :, cols], wd.at[:, :, cols], wsem.at[2, c])
        copy.start()
        down_copies.append(copy)

    ids0, ids1 = ids_ref[0:1, :], ids_ref[1:2, :]
    slot0, slot1 = slot_ref[0:1, :], slot_ref[1:2, :]
    target0 = jnp.where(slot0 >= 0, ids0 * CAP_DEV + slot0, -1)
    target1 = jnp.where(slot1 >= 0, ids1 * CAP_DEV + slot1, -1)
    row = lax.broadcasted_iota(jnp.int32, (slots, ids0.shape[1]), 0)
    placing = jnp.where((row == target0) | (row == target1), 1.0, 0.0).astype(jnp.bfloat16)

    tok_copy.wait()
    first = []
    for c in range(nc):
        cols = pl.ds(c * dc, dc)
        outgoing = jnp.dot(placing, tok[:, cols], preferred_element_type=jnp.float32)
        for x in range(n_cp):
            xs[c, x] = outgoing[x * rpp:(x + 1) * rpp].astype(jnp.bfloat16)
        if c == 0:
            pl.semaphore_wait(barrier, n - 1)
        for j in range(1, n):
            other, where = peer(j)
            copy = pltpu.make_async_remote_copy(
                src_ref=xs.at[c, lax.rem(other, n_cp)],
                dst_ref=xr.at[c, me],
                send_sem=s1.at[c, j],
                recv_sem=r1.at[c, j],
                device_id=where,
                device_id_type=MESH,
            )
            copy.start()
            first.append(copy)
        xr[c, me] = xs[c, my_x]

    rt_copy.wait()
    logits = lax.dot_general(rt[...], tok[...], NT, preferred_element_type=jnp.float32)
    affinity = 1.0 / (1.0 + jnp.exp(-logits))
    erow = lax.broadcasted_iota(jnp.int32, logits.shape, 0)
    chosen0 = jnp.sum(jnp.where(erow == ids0, affinity, 0.0), axis=0, keepdims=True)
    chosen1 = jnp.sum(jnp.where(erow == ids1, affinity, 0.0), axis=0, keepdims=True)
    total = chosen0 + chosen1
    share0 = ROUTE_SCALE * chosen0 / total
    share1 = ROUTE_SCALE * chosen1 / total
    wide = lax.rem(lax.broadcasted_iota(jnp.int32, (n * rpp, ids0.shape[1]), 0), slots)
    mix = jnp.where(wide == target0, share0, 0.0) + jnp.where(wide == target1, share1, 0.0)
    mix = mix.T
    mix_hi = mix.astype(jnp.bfloat16)
    mix_lo = (mix - mix_hi.astype(jnp.float32)).astype(jnp.bfloat16)
    mix_both = jnp.concatenate([mix_hi, mix_lo], axis=0)

    def arrival(buf, c, j, sem):
        source = lax.rem(me + n - j, n)
        ref = buf.at[c, source]
        pltpu.make_async_remote_copy(
            src_ref=ref, dst_ref=ref, send_sem=sem.at[c, j], recv_sem=sem.at[c, j],
            device_id=peer(n - j)[1], device_id_type=MESH,
        ).wait_recv()

    gate = [jnp.zeros((n * rpp, ff), jnp.float32) for _ in range(local)]
    up = [jnp.zeros((n * rpp, ff), jnp.float32) for _ in range(local)]
    for c in range(nc):
        cols = pl.ds(c * dc, dc)
        for copy in up_copies[c]:
            copy.wait()
        for j in range(1, n):
            arrival(xr, c, j, r1)
        x = rows_of(xr, c)
        for e in range(local):
            gate[e] += jnp.dot(x, wg[e, cols, :], preferred_element_type=jnp.float32)
            up[e] += jnp.dot(x, wu[e, cols, :], preferred_element_type=jnp.float32)
    owner = lax.rem(lax.broadcasted_iota(jnp.int32, (n * rpp, ff), 0), rpp) // CAP_DEV
    hidden = []
    for e in range(local):
        value = gate[e] / (1.0 + jnp.exp(-gate[e])) * up[e]
        hidden.append(jnp.where(owner == e, value, 0.0).astype(jnp.bfloat16))

    second = []
    for c in range(nc):
        cols = pl.ds(c * dc, dc)
        down_copies[c].wait()
        part = jnp.dot(hidden[0], wd[0, :, cols], preferred_element_type=jnp.float32)
        for e in range(1, local):
            part += jnp.dot(hidden[e], wd[e, :, cols], preferred_element_type=jnp.float32)
        for i in range(n):
            ps[c, i] = part[i * rpp:(i + 1) * rpp].astype(jnp.bfloat16)
        for j in range(1, n):
            other, where = peer(j)
            copy = pltpu.make_async_remote_copy(
                src_ref=ps.at[c, other],
                dst_ref=pr.at[c, me],
                send_sem=s2.at[c, j],
                recv_sem=r2.at[c, j],
                device_id=where,
                device_id_type=MESH,
            )
            copy.start()
            second.append(copy)
        pr[c, me] = ps[c, me]

    half = mix.shape[0]
    outs = []
    for c in range(nc):
        cols = pl.ds(c * dc, dc)
        for j in range(1, n):
            arrival(pr, c, j, r2)
        both = jnp.dot(mix_both, rows_of(pr, c), preferred_element_type=jnp.float32)
        ob[:, cols] = (both[:half] + both[half:]).astype(jnp.bfloat16)
        copy = pltpu.make_async_copy(ob.at[:, cols], out_hbm.at[:, cols], osem.at[c])
        copy.start()
        outs.append(copy)
    for copy in first + second:
        copy.wait_send()
    for copy in outs:
        copy.wait()


def body(n_tp, n_cp, tokens, router, gate_weight, up_weight, down_weight, expert_ids, slot_index):
    n = n_tp * n_cp
    rows, width = tokens.shape
    local, _, ff = gate_weight.shape
    rpp = local * CAP_DEV
    nc = 4 if n <= 16 else 1
    dc = width // nc
    anywhere = pl.BlockSpec(memory_space=pl.ANY)
    vmem = pl.BlockSpec(memory_space=pltpu.VMEM)
    bf16 = jnp.bfloat16
    dma = pltpu.SemaphoreType.DMA
    return pl.pallas_call(
        functools.partial(kernel, n_tp, n_cp, nc),
        out_shape=jax.ShapeDtypeStruct((rows, width), bf16),
        in_specs=[anywhere, anywhere, vmem, vmem, anywhere, anywhere, anywhere],
        out_specs=anywhere,
        scratch_shapes=[
            pltpu.VMEM((rows, width), bf16),
            pltpu.VMEM((router.shape[1], width), bf16),
            pltpu.VMEM((local, width, ff), bf16),
            pltpu.VMEM((local, width, ff), bf16),
            pltpu.VMEM((local, ff, width), bf16),
            pltpu.VMEM((nc, n_cp, rpp, dc), bf16),
            pltpu.VMEM((nc, n, rpp, dc), bf16),
            pltpu.VMEM((nc, n, rpp, dc), bf16),
            pltpu.VMEM((nc, n, rpp, dc), bf16),
            pltpu.VMEM((rows, width), bf16),
            dma((2,)),
            dma((3, nc)),
            dma((nc,)),
            dma((nc, n)),
            dma((nc, n)),
            dma((nc, n)),
            dma((nc, n)),
        ],
        compiler_params=pltpu.CompilerParams(
            collective_id=0, has_side_effects=True, vmem_limit_bytes=60 * 1024 * 1024
        ),
    )(tokens, router.T, expert_ids.T, slot_index.T, gate_weight, up_weight, down_weight)


def solution(mesh):
    in_specs = (
        P(("dp", "tp", "cp"), None),
        P(),
        P("cp", None, "tp"),
        P("cp", None, "tp"),
        P("cp", "tp", None),
        P(("dp", "tp", "cp"), None),
        P(("dp", "tp", "cp"), None),
    )
    out_specs = P(("dp", "tp", "cp"), None)
    step = functools.partial(body, mesh.shape["tp"], mesh.shape["cp"])
    return jax.shard_map(step, mesh=mesh, in_specs=in_specs, out_specs=out_specs, check_vma=False)
```

time: 57.7 us -> 33.5 us (0.58)
  blocking collectives: 36.6 us -> 0 us
  Pallas kernels: 0 us -> 31.2 us
  matrix products: 15.4 us -> 0 us
  other arithmetic: 1.96 us -> 0 us
  local copies, waits for them, and re-layouts: 3.42 us -> 2.16 us
    all_to_all x2 -> x0, blocking collectives: 36.6 us -> none  [the longest x1 20.3 us: body(): lax.all_to_all(copies, ('tp', 'cp'), split_axis=0, concat_axis=0, tiled=T...]
    pallas_call x0 -> x1, Pallas kernels: none -> 31.2 us  [body(): pl.pallas_call(functools.partial(kernel, n_tp, n_cp, nc), out_shape=jax.S...]
    dot_general x5 -> x0, matrix products: 15.4 us -> none  [the longest x1 7.26 us: body(): jnp.einsum('esf,efd->esd', hidden, down_weight, preferred_element_type=jn...]
    unnamed x4 -> x1, local copies, waits for them, and re-layouts: 0.01 us -> 2.16 us
    gather x5 -> x0, local copies, waits for them, and re-layouts: 1.97 us -> none  [body(): chosen = jnp.take_along_axis(affinity, expert_ids, axis=1)]
    reshape x4 -> x0, local copies, waits for them, and re-layouts: 0.83 us -> none  [the longest x2 0.5 us: body(): partial_value = jnp.einsum('esf,efd->esd', hidden, down_weight, preferred...]
    gather x1 -> x0, other arithmetic: 0.77 us -> none  [body(): chosen = jnp.take_along_axis(affinity, expert_ids, axis=1)]
    select_n x1 -> x0, other arithmetic: 0.7 us -> none  [body(): target = jnp.where(slot_index >= 0, expert_ids * CAP_DEV + slot_index, -1)]
where the time goes in v1:
time: 33.5 us; the launch traced here: 33.3 us
  Pallas kernels  31.2 us (93%)
  local copies, waits for them, and re-layouts  2.16 us (6%)
    pallas_call x1, Pallas kernels, body(): pl.pallas_call(functools.partial(kernel, n_tp, n_cp, nc), out_shape=jax.S...  31.2 us
    unnamed x1, local copies, waits for them, and re-layouts  2.16 us

profile of v1, /device:TPU:0, one launch (start us, length us, event | category | flops | bytes accessed | tf_op | source)
XLA Modules:
  0.0 33.3 jit_solution(2602615090972886301)
XLA Ops:
  0.0 31.2 %shard_map.73 = bf16[64,7168]{1,0:T(8,128)(2,1)} custom-call(bf16[64,7168]{1,0:T(8,128)(2,1)} %tok_hbm.1, bf16[4,7168]{1,0:T(4,128)(2,1)} %bitcast.3, s32[2,64]{1,0:T(2,128)} %bitcast.4, s32[2,64]{1,0:T(2,128)} %bitcast.5, bf16[2,7168,256]{2,1,0:T(8,128)(2,1)} %wg_hbm.1, bf16[2,7168,256]{2,1,0:T(8,128)(2,1)} %wu_hbm.1, bf16[2,256,7168]{2,1,0:T(8,128)(2,1)} %wd_hbm.1), custom_call_target="tpu_custom_call" | custom-call | tf_op jit(solution)/shard_map/pallas_call | solution.py:189
  31.2 2.2 %copy.9 = bf16[64,7168]{1,0:T(8,128)(2,1)} copy(bf16[64,7168]{1,0:T(8,128)(2,1)} %shard_map.73) | data formatting | bytes 1835008

commit v2 on v0

v2 whole, which is shorter than its diff:
```python
import functools

import jax
import jax.numpy as jnp
from jax import lax
from jax.experimental import pallas as pl
from jax.experimental.pallas import tpu as pltpu
from jax.sharding import PartitionSpec as P

CAP_DEV = 2
ROUTE_SCALE = 2.5
CHUNKS = 1
MESH = pl.DeviceIdType.MESH
NT = (((1,), (1,)), ((), ()))


def rows_of(pieces):
    return jnp.concatenate([p.astype(jnp.float32) for p in pieces], axis=0).astype(jnp.bfloat16)


def flip(index, bits):
    for b in range(bits.bit_length()):
        if (bits >> b) & 1:
            index = index + (1 - 2 * lax.rem(index // (1 << b), 2)) * (1 << b)
    return index


def exchange_kernel(
    n_tp, n_cp, nc,
    tok_hbm, rt_hbm, ids_hbm, slot_hbm, wg_hbm, wu_hbm, wd_hbm,
    pr, mix_hbm,
    ids_ref, slot_ref, tok, rt, wg, wu, wd, xs, xr, ps, mix_ref,
    in_sem, wsem, own_sem, s1, r1, s2, r2,
):
    n = n_tp * n_cp
    my_z, my_x = lax.axis_index("tp"), lax.axis_index("cp")
    me = my_z * n_cp + my_x
    local, width, ff = wg.shape
    dc = width // nc
    slots = n_cp * local * CAP_DEV
    pow2 = n & (n - 1) == 0
    order = list(range(n - 1, 0, -1))

    def peer(j):
        return flip(me, j) if pow2 else lax.rem(me + j, n)

    def source(j):
        return flip(me, j) if pow2 else lax.rem(me + n - j, n)

    def device(other):
        return {"tp": other // n_cp, "cp": lax.rem(other, n_cp)}

    index_copies = [
        pltpu.make_async_copy(ids_hbm, ids_ref, in_sem.at[nc + 2]),
        pltpu.make_async_copy(slot_hbm, slot_ref, in_sem.at[nc + 3]),
    ]
    for copy in index_copies:
        copy.start()
    tok_copies = []
    for c in range(nc):
        cols = pl.ds(c * dc, dc)
        copy = pltpu.make_async_copy(tok_hbm.at[:, cols], tok.at[:, cols], in_sem.at[c])
        copy.start()
        tok_copies.append(copy)
    rt_copy = pltpu.make_async_copy(rt_hbm, rt, in_sem.at[nc])
    rt_copy.start()

    barrier = pltpu.get_barrier_semaphore()
    for j in order:
        pl.semaphore_signal(barrier, inc=1, device_id=device(peer(j)), device_id_type=MESH)

    up_copies, down_copies = {}, {}
    for e in range(local):
        for c in range(nc):
            cols = pl.ds(c * dc, dc)
            pair = [
                pltpu.make_async_copy(wg_hbm.at[e, cols, :], wg.at[e, cols, :], wsem.at[0, e, c]),
                pltpu.make_async_copy(wu_hbm.at[e, cols, :], wu.at[e, cols, :], wsem.at[1, e, c]),
            ]
            for copy in pair:
                copy.start()
            up_copies[e, c] = pair
        for c in range(nc):
            cols = pl.ds(c * dc, dc)
            copy = pltpu.make_async_copy(wd_hbm.at[e, :, cols], wd.at[e, :, cols], wsem.at[2, e, c])
            copy.start()
            down_copies[e, c] = copy

    for copy in index_copies:
        copy.wait()
    ids0, ids1 = ids_ref[0:1, :], ids_ref[1:2, :]
    slot0, slot1 = slot_ref[0:1, :], slot_ref[1:2, :]
    target0 = jnp.where(slot0 >= 0, ids0 * CAP_DEV + slot0, -1)
    target1 = jnp.where(slot1 >= 0, ids1 * CAP_DEV + slot1, -1)
    row = lax.broadcasted_iota(jnp.int32, (slots, ids0.shape[1]), 0)
    placing = jnp.where((row == target0) | (row == target1), 1.0, 0.0).astype(jnp.bfloat16)

    sends = []

    def dispatch(e, c):
        for j in order:
            other = peer(j)
            copy = pltpu.make_async_remote_copy(
                src_ref=xs.at[e, c, lax.rem(other, n_cp)],
                dst_ref=xr.at[e, c, me],
                send_sem=s1.at[e, c, j],
                recv_sem=r1.at[e, c, j],
                device_id=device(other),
                device_id_type=MESH,
            )
            copy.start()
            sends.append(copy)
        xr[e, c, me] = xs[e, c, my_x]

    for c in range(nc):
        tok_copies[c].wait()
        cols = pl.ds(c * dc, dc)
        outgoing = jnp.dot(placing, tok[:, cols], preferred_element_type=jnp.float32)
        for x in range(n_cp):
            for e in range(local):
                at = (x * local + e) * CAP_DEV
                xs[e, c, x] = outgoing[at:at + CAP_DEV].astype(jnp.bfloat16)
        if c == 0:
            pl.semaphore_wait(barrier, n - 1)
        dispatch(0, c)
    for e in range(1, local):
        for c in range(nc):
            dispatch(e, c)

    rt_copy.wait()
    logits = lax.dot_general(rt[...], tok[...], NT, preferred_element_type=jnp.float32)
    affinity = 1.0 / (1.0 + jnp.exp(-logits))
    erow = lax.broadcasted_iota(jnp.int32, logits.shape, 0)
    chosen0 = jnp.sum(jnp.where(erow == ids0, affinity, 0.0), axis=0, keepdims=True)
    chosen1 = jnp.sum(jnp.where(erow == ids1, affinity, 0.0), axis=0, keepdims=True)
    total = chosen0 + chosen1
    share0 = ROUTE_SCALE * chosen0 / total
    share1 = ROUTE_SCALE * chosen1 / total
    wide = lax.broadcasted_iota(jnp.int32, (local * n * CAP_DEV, ids0.shape[1]), 0)
    which = lax.rem(wide // CAP_DEV, n_cp) * local + wide // (n * CAP_DEV)
    wide = which * CAP_DEV + lax.rem(wide, CAP_DEV)
    mix = jnp.where(wide == target0, share0, 0.0) + jnp.where(wide == target1, share1, 0.0)
    mix = mix.T
    mix_hi = mix.astype(jnp.bfloat16)
    mix_lo = (mix - mix_hi.astype(jnp.float32)).astype(jnp.bfloat16)
    mix_ref[...] = jnp.concatenate([mix_hi, mix_lo], axis=0)
    mix_copy = pltpu.make_async_copy(mix_ref, mix_hbm, in_sem.at[nc + 1])
    mix_copy.start()

    def arrival(ref, j, sem):
        pltpu.make_async_remote_copy(
            src_ref=ref, dst_ref=ref, send_sem=sem, recv_sem=sem,
            device_id=device(peer(j)), device_id_type=MESH,
        ).wait_recv()

    owns = []
    for e in range(local):
        gate = jnp.zeros((n * CAP_DEV, ff), jnp.float32)
        up = jnp.zeros((n * CAP_DEV, ff), jnp.float32)
        for c in range(nc):
            cols = pl.ds(c * dc, dc)
            for copy in up_copies[e, c]:
                copy.wait()
            for j in order:
                arrival(xr.at[e, c, source(j)], j, r1.at[e, c, j])
            x = rows_of([xr[e, c, i] for i in range(n)])
            gate += jnp.dot(x, wg[e, cols, :], preferred_element_type=jnp.float32)
            up += jnp.dot(x, wu[e, cols, :], preferred_element_type=jnp.float32)
        hidden = (gate / (1.0 + jnp.exp(-gate)) * up).astype(jnp.bfloat16)
        for c in range(nc):
            cols = pl.ds(c * dc, dc)
            down_copies[e, c].wait()
            part = jnp.dot(hidden, wd[e, :, cols], preferred_element_type=jnp.float32)
            for i in range(n):
                ps[e, c, i] = part[i * CAP_DEV:(i + 1) * CAP_DEV].astype(jnp.bfloat16)
            for j in order:
                other = peer(j)
                copy = pltpu.make_async_remote_copy(
                    src_ref=ps.at[e, c, other],
                    dst_ref=pr.at[e, c, me],
                    send_sem=s2.at[e, c, j],
                    recv_sem=r2.at[e, c, j],
                    device_id=device(other),
                    device_id_type=MESH,
                )
                copy.start()
                sends.append(copy)
            own = pltpu.make_async_copy(ps.at[e, c, me], pr.at[e, c, me], own_sem.at[e, c])
            own.start()
            owns.append(own)
    mix_copy.wait()
    for copy in owns:
        copy.wait()
    for copy in sends:
        copy.wait_send()
    for e in range(local):
        for c in range(nc):
            for j in order:
                arrival(pr.at[e, c, source(j)], j, r2.at[e, c, j])


def combine_kernel(pr_hbm, mix_hbm, out_hbm, pr, mix_ref, ob, isem, osem):
    local, nc, n, cap, dc = pr.shape
    mix_copy = pltpu.make_async_copy(mix_hbm, mix_ref, isem.at[nc])
    mix_copy.start()
    loads, outs = [], []
    for c in range(nc):
        copy = pltpu.make_async_copy(pr_hbm.at[:, c], pr.at[:, c], isem.at[c])
        copy.start()
        loads.append(copy)
    mix_copy.wait()
    mix = mix_ref[...]
    half = mix.shape[0] // 2
    for c in range(nc):
        loads[c].wait()
        rows = rows_of([pr[e, c, i] for e in range(local) for i in range(n)])
        for p in range(2):
            part = dc // 2
            cols = pl.ds(c * dc + p * part, part)
            both = jnp.dot(
                mix, rows[:, p * part:(p + 1) * part], preferred_element_type=jnp.float32
            )
            ob[:, cols] = (both[:half] + both[half:]).astype(jnp.bfloat16)
            copy = pltpu.make_async_copy(ob.at[:, cols], out_hbm.at[:, cols], osem.at[c, p])
            copy.start()
            outs.append(copy)
    for copy in outs:
        copy.wait()


def body(n_tp, n_cp, tokens, router, gate_weight, up_weight, down_weight, expert_ids, slot_index):
    n = n_tp * n_cp
    rows, width = tokens.shape
    local, _, ff = gate_weight.shape
    nc = CHUNKS if n <= 16 else 1
    dc = width // nc
    anywhere = pl.BlockSpec(memory_space=pl.ANY)
    bf16 = jnp.bfloat16
    dma = pltpu.SemaphoreType.DMA
    slab = (local, nc, n, CAP_DEV, dc)
    pr, mix = pl.pallas_call(
        functools.partial(exchange_kernel, n_tp, n_cp, nc),
        out_shape=[
            jax.ShapeDtypeStruct(slab, bf16),
            jax.ShapeDtypeStruct((2 * rows, local * n * CAP_DEV), bf16),
        ],
        in_specs=[anywhere] * 7,
        out_specs=[anywhere, anywhere],
        scratch_shapes=[
            pltpu.VMEM((expert_ids.shape[1], rows), jnp.int32),
            pltpu.VMEM((slot_index.shape[1], rows), jnp.int32),
            pltpu.VMEM((rows, width), bf16),
            pltpu.VMEM((router.shape[1], width), bf16),
            pltpu.VMEM((local, width, ff), bf16),
            pltpu.VMEM((local, width, ff), bf16),
            pltpu.VMEM((local, ff, width), bf16),
            pltpu.VMEM((local, nc, n_cp, CAP_DEV, dc), bf16),
            pltpu.VMEM(slab, bf16),
            pltpu.VMEM(slab, bf16),
            pltpu.VMEM((2 * rows, local * n * CAP_DEV), bf16),
            dma((nc + 4,)),
            dma((3, local, nc)),
            dma((local, nc)),
            dma((local, nc, n)),
            dma((local, nc, n)),
            dma((local, nc, n)),
            dma((local, nc, n)),
        ],
        compiler_params=pltpu.CompilerParams(
            collective_id=0, has_side_effects=True, vmem_limit_bytes=60 * 1024 * 1024
        ),
    )(tokens, router.T, expert_ids.T, slot_index.T, gate_weight, up_weight, down_weight)
    return pl.pallas_call(
        combine_kernel,
        out_shape=jax.ShapeDtypeStruct((rows, width), bf16),
        in_specs=[anywhere, anywhere],
        out_specs=anywhere,
        scratch_shapes=[
            pltpu.VMEM(slab, bf16),
            pltpu.VMEM(mix.shape, bf16),
            pltpu.VMEM((rows, width), bf16),
            dma((nc + 1,)),
            dma((nc, 2)),
        ],
    )(pr, mix)


def solution(mesh):
    in_specs = (
        P(("dp", "tp", "cp"), None),
        P(),
        P("cp", None, "tp"),
        P("cp", None, "tp"),
        P("cp", "tp", None),
        P(("dp", "tp", "cp"), None),
        P(("dp", "tp", "cp"), None),
    )
    out_specs = P(("dp", "tp", "cp"), None)
    step = functools.partial(body, mesh.shape["tp"], mesh.shape["cp"])
    return jax.shard_map(step, mesh=mesh, in_specs=in_specs, out_specs=out_specs, check_vma=False)
```

time: 57.7 us -> 30.1 us (0.52)
  blocking collectives: 36.6 us -> 0 us
  Pallas kernels: 0 us -> 29.9 us
  matrix products: 15.4 us -> 0 us
  local copies, waits for them, and re-layouts: 3.42 us -> 0 us
  other arithmetic: 1.96 us -> 0 us
    all_to_all x2 -> x0, blocking collectives: 36.6 us -> none  [the longest x1 20.3 us: body(): lax.all_to_all(copies, ('tp', 'cp'), split_axis=0, concat_axis=0, tiled=T...]
    pallas_call x0 -> x2, Pallas kernels: none -> 29.9 us  [the longest x1 27.4 us: body(): pl.pallas_call(functools.partial(exchange_kernel, n_tp, n_cp, nc), out_sh...]
    dot_general x5 -> x0, matrix products: 15.4 us -> none  [the longest x1 7.26 us: body(): jnp.einsum('esf,efd->esd', hidden, down_weight, preferred_element_type=jn...]
    gather x5 -> x0, local copies, waits for them, and re-layouts: 1.97 us -> none  [body(): chosen = jnp.take_along_axis(affinity, expert_ids, axis=1)]
    reshape x4 -> x0, local copies, waits for them, and re-layouts: 0.83 us -> none  [the longest x2 0.5 us: body(): partial_value = jnp.einsum('esf,efd->esd', hidden, down_weight, preferred...]
    gather x1 -> x0, other arithmetic: 0.77 us -> none  [body(): chosen = jnp.take_along_axis(affinity, expert_ids, axis=1)]
    select_n x1 -> x0, other arithmetic: 0.7 us -> none  [body(): target = jnp.where(slot_index >= 0, expert_ids * CAP_DEV + slot_index, -1)]
where the time goes in v2:
time: 30.1 us; the launch traced here: 29.9 us
  Pallas kernels  29.9 us (99%)
    pallas_call x1, Pallas kernels, body(): pl.pallas_call(functools.partial(exchange_kernel, n_tp, n_cp, nc), out_sh...  27.4 us
    pallas_call x1, Pallas kernels, body(): pl.pallas_call(combine_kernel, out_shape=jax.ShapeDtypeStruct((rows, widt...  2.49 us

profile of v2, /device:TPU:0, one launch (start us, length us, event | category | flops | bytes accessed | tf_op | source)
XLA Modules:
  0.0 29.9 jit_solution(10503813464888287399)
XLA Ops:
  0.0 27.4 %shard_map.73 = (bf16[2,1,8,2,7168]{4,3,2,1,0:T(2,128)(2,1)}, bf16[128,32]{1,0:T(8,128)(2,1)}) custom-call(bf16[64,7168]{1,0:T(8,128)(2,1)} %tok_hbm.1, bf16[4,7168]{1,0:T(4,128)(2,1)} %bitcast.3, s32[2,64]{1,0:T(2,128)} %bitcast.4, s32[2,64]{1,0:T(2,128)} %bitcast.5, bf16[2,7168,256]{2,1,0:T(8,128)(2,1)} %wg_hbm.1, bf16[2,7168,256]{2,1,0:T(8,128)(2,1)} %wu_hbm.1, ...), custom_call_target="tpu_custom_call" | custom-call | tf_op jit(solution)/shard_map/pallas_call | solution.py:241
  27.4 2.5 %shard_map.74 = bf16[64,7168]{1,0:T(8,128)(2,1)} custom-call(bf16[2,1,8,2,7168]{4,3,2,1,0:T(2,128)(2,1)} %get-tuple-element.7.pr_hbm, bf16[128,32]{1,0:T(8,128)(2,1)} %get-tuple-element.8.mix_hbm), custom_call_target="tpu_custom_call" | custom-call | tf_op jit(solution)/shard_map/pallas_call | solution.py:273
